TPU v7x, 32 devices: a whole 2x2x4 slice. The times are simulated.
32 devices in a mesh: tp: 8 (over z, y), dp: 4 (over x, core).
Axes of the slice: x: 2, y: 2, z: 4, core: 2. Of those that a mesh axis runs over, the one named last changes fastest.
Arguments:
- tokens: bfloat16 [768, 4096], P(('dp', 'tp')), may hold values from -6 to 6
- hidden_grad: bfloat16 [768, 14336], P('dp', 'tp'), may hold values from -0.59765625 to 0.59765625
- gate_value: bfloat16 [768, 14336], P('dp', 'tp'), may hold values from -6 to 6
- up_value: bfloat16 [768, 14336], P('dp', 'tp'), may hold values from -6 to 6
- gate_weight: bfloat16 [4096, 14336], P('dp', 'tp'), may hold values from -0.09375 to 0.09375
- up_weight: bfloat16 [4096, 14336], P('dp', 'tp'), may hold values from -0.09375 to 0.09375
Outputs:
- input_grad: bfloat16 [768, 4096], P(('dp', 'tp'))
- gate_grad: bfloat16 [4096, 14336], P('dp', 'tp')
- up_grad: bfloat16 [4096, 14336], P('dp', 'tp')
All inputs are finite; a program needn't handle non-finite values.
Results may differ from a plain program's by a relative error of at most 0.018.
Values may be sent and summed in bfloat16 or wider, within the bound.
A program may use at most 128 MiB of HBM per device.

v0:
```python
import jax
import jax.numpy as jnp
from jax import lax
from jax.sharding import PartitionSpec as P


def on_device(tokens, hidden_grad, gate_value, up_value, gate_weight, up_weight):
    n_dp = lax.axis_size("dp")
    n_tp = lax.axis_size("tp")
    token_rows, features = tokens.shape
    width = gate_weight.shape[0]
    hidden_width = gate_value.shape[1]
    gate_float = gate_value.astype(jnp.float32)
    up_float = up_value.astype(jnp.float32)
    logistic = jax.nn.sigmoid(gate_float)
    upstream = hidden_grad.astype(jnp.float32)
    d_gate = (upstream * up_float * logistic * (1.0 + gate_float * (1.0 - logistic))).astype(
        jnp.bfloat16
    )
    d_up = (upstream * gate_float * logistic).astype(jnp.bfloat16)
    pieces = lax.all_gather(jnp.concatenate([d_gate, d_up], axis=1), "dp", axis=0, tiled=True)
    mine = lax.all_to_all(tokens, "dp", split_axis=1, concat_axis=0, tiled=True)
    columns = lax.all_gather(mine, "tp", axis=0, tiled=True)
    columns = columns.reshape(n_tp, n_dp, token_rows, width).transpose(1, 0, 2, 3)
    columns = columns.reshape(n_tp * n_dp * token_rows, width)
    across = (((1,), (1,)), ((), ()))
    contract = (((0,), (0,)), ((), ()))
    partial = (
        lax.dot_general(
            pieces[:, :hidden_width], gate_weight, across, preferred_element_type=jnp.float32
        )
        + lax.dot_general(
            pieces[:, hidden_width:], up_weight, across, preferred_element_type=jnp.float32
        )
    ).astype(jnp.bfloat16)
    partial = partial.reshape(n_dp, n_tp, token_rows, width).transpose(1, 0, 2, 3)
    partial = partial.reshape(n_tp * n_dp * token_rows, width)
    summed = lax.psum_scatter(partial, "tp", scatter_dimension=0, tiled=True)
    input_grad = lax.all_to_all(summed, "dp", split_axis=0, concat_axis=1, tiled=True)
    gate_grad = lax.dot_general(
        columns, pieces[:, :hidden_width], contract, preferred_element_type=jnp.float32
    ).astype(jnp.bfloat16)
    up_grad = lax.dot_general(
        columns, pieces[:, hidden_width:], contract, preferred_element_type=jnp.float32
    ).astype(jnp.bfloat16)
    return (input_grad, gate_grad, up_grad)


def solution(mesh):
    placed = (
        P(("dp", "tp"), None),
        P("dp", "tp"),
        P("dp", "tp"),
        P("dp", "tp"),
        P("dp", "tp"),
        P("dp", "tp"),
    )
    return jax.shard_map(
        on_device,
        mesh=mesh,
        in_specs=placed,
        out_specs=(P(("dp", "tp"), None), P("dp", "tp"), P("dp", "tp")),
        check_vma=False,
    )
```

profile of v0, /device:TPU:0, one launch (start us, length us, event | category | flops | bytes accessed | tf_op | source)
XLA Modules:
  0.0 198.5 jit_solution(8815059297840828324)
XLA Ops:
  7.2 0.0 all-gather.3.cloned.1.call-start
  7.2 2.2 %fusion.12 = (bf16[192,1792]{1,0:T(8,128)(2,1)S(1)}, bf16[192,1792]{1,0:T(8,128)(2,1)S(1)}) fusion(bf16[192,1792]{1,0:T(8,128)(2,1)} %param.7, bf16[192,1792]{1,0:T(8,128)(2,1)} %param.8, bf16[192,1792]{1,0:T(8,128)(2,1)} %param.9), kind=kLoop, calls=%fused_computation.17 | loop fusion | flops 5505024 | bytes 3440640 | tf_op jit(solution)/shard_map/convert_element_type | solution.py:17
  9.4 0.0 copy-start
  9.5 1.2 pad_maximum_fusion
  10.6 0.0 all-gather.3.cloned.1.call-update
  10.6 0.0 all-gather.5.cloned.1.call-start
  10.7 9.4 %all_to_all.38 = bf16[24,4,1024]{2,0,1:T(8,128)(2,1)} all-to-all(bf16[24,4,1024]{2,0,1:T(8,128)(2,1)S(1)} %bitcast.34), channel_id=1, replica_groups=mesh['tp'=8,'dp'=4] {'dp'}, dimensions={1} | all-to-all | bytes 393216 | tf_op jit(solution)/shard_map/all_to_all | solution.py:22
  20.2 0.0 all-gather.5.cloned.1.call-update
  20.2 0.0 reduce-scatter.2.cloned.1.call-start
  20.2 35.2 %all-gather.3.cloned.1.call-done = bf16[768,3584]{1,0:T(8,128)(2,1)} async-done(((bf16[192,3584]{1,0:T(8,128)(2,1)}), bf16[768,3584]{1,0:T(8,128)(2,1)}) %all-gather.3.cloned.1.call-update) | async-done | bytes 5505040 | tf_op jit(solution)/shard_map/all_gather | solution.py:21
  55.4 6.0 %fusion.3 = f32[768,1024]{1,0:T(8,128)S(1)} fusion(bf16[1024,1792]{1,0:T(8,128)(2,1)} %param.11, bf16[768,3584]{1,0:T(8,128)(2,1)} %all-gather.3.cloned.1.call-done), kind=kOutput, calls=%fused_computation.6 | convolution fusion | flops 2818572288 | bytes 9568256 | tf_op jit(solution)/shard_map/dot_general | solution.py:32
  61.5 3.0 %add_convert_fusion = bf16[768,1024]{1,0:T(8,128)(2,1)S(1)} fusion(f32[768,1024]{1,0:T(8,128)S(1)} %fusion.3, bf16[1024,1792]{1,0:T(8,128)(2,1)S(1)} %copy-done.2, bf16[768,3584]{1,0:T(8,128)(2,1)S(1)} %copy-done.1), kind=kOutput, calls=%fused_computation.4 | convolution fusion | flops 2820145152 | bytes 11141120 | tf_op jit(solution)/shard_map/dot_general | solution.py:29
  64.5 1.3 copy.21
  65.8 0.0 reduce-scatter.2.cloned.1.call-update
  65.8 36.0 %all-gather.5.cloned.1.call-done = bf16[768,1024]{1,0:T(8,128)(2,1)} async-done(((bf16[96,1024]{1,0:T(8,128)(2,1)}), bf16[768,1024]{1,0:T(8,128)(2,1)}) %all-gather.5.cloned.1.call-update) | async-done | bytes 1572880 | tf_op jit(solution)/shard_map/all_gather | solution.py:23
  101.8 1.6 copy.24
  103.4 6.4 %fusion = bf16[1024,1792]{0,1:T(8,128)(2,1)} fusion(bf16[768,1024]{1,0:T(8,128)(2,1)S(1)} %bitcast.29, bf16[768,3584]{1,0:T(8,128)(2,1)} %all-gather.3.cloned.1.call-done), kind=kOutput, calls=%fused_computation.2 | convolution fusion | flops 2820407296 | bytes 7995392 | tf_op jit(solution)/shard_map/dot_general | solution.py:40
  109.8 60.0 %reduce-scatter.2.cloned.1.call-done = bf16[96,1024]{1,0:T(8,128)(2,1)} async-done(((bf16[768,1024]{1,0:T(8,128)(2,1)}), bf16[96,1024]{1,0:T(8,128)(2,1)}) %reduce-scatter.2.cloned.1.call-update) | async-done | bytes 196624 | tf_op jit(solution)/shard_map/reduce_scatter | solution.py:38
  169.8 3.4 %all-to-all-start = ((bf16[4,24,1024]{2,1,0:T(8,128)(2,1)}), bf16[4,24,1024]{2,1,0:T(8,128)(2,1)S(1)}, u32[]{:S(2)}, u32[]{:S(2)}) async-start(bf16[4,24,1024]{2,1,0:T(8,128)(2,1)} %bitcast.36), calls=%async_computation.1 | async-start | bytes 393216 | tf_op jit(solution)/shard_map/all_to_all | solution.py:39
  173.1 6.3 %fusion.1 = bf16[1024,1792]{0,1:T(8,128)(2,1)} fusion(bf16[768,1024]{1,0:T(8,128)(2,1)S(1)} %bitcast.30, bf16[768,3584]{1,0:T(8,128)(2,1)} %all-gather.3.cloned.1.call-done), kind=kOutput, calls=%fused_computation.3 | convolution fusion | flops 2820407296 | bytes 7995392 | tf_op jit(solution)/shard_map/dot_general | solution.py:43
  179.4 5.9 %copy.26 = bf16[1024,1792]{1,0:T(8,128)(2,1)} copy(bf16[1024,1792]{0,1:T(8,128)(2,1)} %fusion.1) | data formatting | bytes 7340032
  185.3 5.9 %copy.25 = bf16[1024,1792]{1,0:T(8,128)(2,1)} copy(bf16[1024,1792]{0,1:T(8,128)(2,1)} %fusion) | data formatting | bytes 7340032
  191.3 0.0 all-to-all-done
  191.3 0.7 copy.28
  (6 shorter events, 0.0 us)
Async XLA Ops:
  7.2 48.3 %all-gather.3.cloned.1.call-start = ((), (), s32[]{:S(2)}) async-start(), calls=%async_computation.3 | async-start | bytes 6881280 | tf_op jit(solution)/shard_map/all_gather | solution.py:21
  9.4 1.3 copy-start
  10.6 91.2 %all-gather.5.cloned.1.call-start = ((), (), s32[]{:S(2)}) async-start(), calls=%async_computation.5 | async-start | bytes 1769472 | tf_op jit(solution)/shard_map/all_gather | solution.py:23
  20.2 149.6 %reduce-scatter.2.cloned.1.call-start = ((), (), s32[]{:S(2)}) async-start(), calls=%async_computation.4 | async-start | bytes 1769472 | tf_op jit(solution)/shard_map/reduce_scatter | solution.py:38
  55.4 6.1 %copy-start.1 = (bf16[768,3584]{1,0:T(8,128)(2,1)S(1)}, bf16[768,3584]{1,0:T(8,128)(2,1)}, u32[]{:S(2)}) copy-start(bf16[768,3584]{1,0:T(8,128)(2,1)} %all-gather.3.cloned.1.call-done) | copy-start | bytes 16515076
  55.4 6.1 %copy-start.2 = (bf16[1024,1792]{1,0:T(8,128)(2,1)S(1)}, bf16[1024,1792]{1,0:T(8,128)(2,1)}, u32[]{:S(2)}) copy-start(bf16[1024,1792]{1,0:T(8,128)(2,1)} %param.10) | copy-start | bytes 11010052
  169.8 21.5 %all-to-all-start = ((bf16[4,24,1024]{2,1,0:T(8,128)(2,1)}), bf16[4,24,1024]{2,1,0:T(8,128)(2,1)S(1)}, u32[]{:S(2)}, u32[]{:S(2)}) async-start(bf16[4,24,1024]{2,1,0:T(8,128)(2,1)} %bitcast.36), calls=%async_computation.1 | async-start | bytes 393216 | tf_op jit(solution)/shard_map/all_to_all | solution.py:39
Sparse Core Ops, SparseCore 0:
  10.8 44.6 all-gather.2
  57.6 44.1 all-gather.4
  105.8 63.8 reduce-scatter.1
where the time goes:
time: 199 us; the launch traced here: 198 us
  waiting for transfers between devices  131 us (66%)
  matrix products  21.8 us (11%)
  local copies, waits for them, and re-layouts  15.4 us (8%)
  between operations  13.8 us (7%)
  blocking collectives  9.44 us (5%)
  starting transfers between devices  3.49 us (2%)
  other arithmetic  3.4 us (2%)
    reduce_scatter x1, waiting for transfers between devices, on_device(): summed = lax.psum_scatter(partial, 'tp', scatter_dimension=0, tiled=True)  60 us
    all_gather x1, waiting for transfers between devices, on_device(): columns = lax.all_gather(mine, 'tp', axis=0, tiled=True)  36 us
    all_gather x1, waiting for transfers between devices, on_device(): lax.all_gather(jnp.concatenate([d_gate, d_up], axis=1), 'dp', axis=0, til...  35.2 us
    unnamed x8, local copies, waits for them, and re-layouts  11.8 us
    all_to_all x1, blocking collectives, on_device(): mine = lax.all_to_all(tokens, 'dp', split_axis=1, concat_axis=0, tiled=True)  9.44 us
    dot_general x1, matrix products, on_device(): lax.dot_general(columns, pieces[:, :hidden_width], contract, preferred_el...  6.42 us
    dot_general x1, matrix products, on_device(): lax.dot_general(columns, pieces[:, hidden_width:], contract, preferred_el...  6.3 us
    dot_general x1, matrix products, on_device(): lax.dot_general(pieces[:, hidden_width:], up_weight, across, preferred_el...  6.04 us
  transfers between devices with their start and end apart: 4, of which 3 were waited for; matrix products, arithmetic and copies ran while one was open for 18% of the time, Pallas kernels for 0%

commit v1 on v0

--- a/solution.py
+++ b/solution.py
@@ -20,7 +20,8 @@
     d_up = (upstream * gate_float * logistic).astype(jnp.bfloat16)
     pieces = lax.all_gather(jnp.concatenate([d_gate, d_up], axis=1), "dp", axis=0, tiled=True)
     mine = lax.all_to_all(tokens, "dp", split_axis=1, concat_axis=0, tiled=True)
-    columns = lax.all_gather(mine, "tp", axis=0, tiled=True)
+    sent = jnp.stack([mine] * lax.axis_size("tp"))
+    columns = jnp.concatenate(lax.all_to_all(sent, "tp", 0, 0), axis=0)
     columns = columns.reshape(n_tp, n_dp, token_rows, width).transpose(1, 0, 2, 3)
     columns = columns.reshape(n_tp * n_dp * token_rows, width)
     across = (((1,), (1,)), ((), ()))

time: 199 us -> 161 us (0.81)
  waiting for transfers between devices: 131 us -> 87.3 us
  starting transfers between devices: 3.49 us -> 9.27 us
    all_gather x1 -> x0, waiting for transfers between devices: 36 us -> none  [on_device(): columns = lax.all_gather(mine, 'tp', axis=0, tiled=True)]
    all_gather x1, waiting for transfers between devices: 35.2 us -> 28.2 us  [on_device(): lax.all_gather(jnp.concatenate([d_gate, d_up], axis=1), 'dp', axis=0, til...]
    all_to_all x0 -> x1, starting transfers between devices: none -> 5.83 us  [on_device(): columns = jnp.concatenate(lax.all_to_all(sent, 'tp', 0, 0), axis=0)]
  transfers between devices with their start and end apart: 4 -> 4, of which waited for: 3 -> 2; matrix products, arithmetic and copies ran while one was open for 18% -> 23% of each run, Pallas kernels for 0% -> 0%
where the time goes in v1:
time: 161 us
  waiting for transfers between devices  87.3 us (54%)
  matrix products  21.8 us (14%)
  local copies, waits for them, and re-layouts  15.3 us (10%)
  between operations  14.1 us (9%)
  blocking collectives  9.34 us (6%)
  starting transfers between devices  9.27 us (6%)
  other arithmetic  3.4 us (2%)
    reduce_scatter x1, waiting for transfers between devices, on_device(): summed = lax.psum_scatter(partial, 'tp', scatter_dimension=0, tiled=True)  59.1 us
    all_gather x1, waiting for transfers between devices, on_device(): lax.all_gather(jnp.concatenate([d_gate, d_up], axis=1), 'dp', axis=0, til...  28.2 us
    unnamed x8, local copies, waits for them, and re-layouts  11.8 us
    all_to_all x1, blocking collectives, on_device(): mine = lax.all_to_all(tokens, 'dp', split_axis=1, concat_axis=0, tiled=True)  9.34 us
    dot_general x1, matrix products, on_device(): lax.dot_general(columns, pieces[:, :hidden_width], contract, preferred_el...  6.42 us
    dot_general x1, matrix products, on_device(): lax.dot_general(columns, pieces[:, hidden_width:], contract, preferred_el...  6.3 us
    dot_general x1, matrix products, on_device(): lax.dot_general(pieces[:, hidden_width:], up_weight, across, preferred_el...  6.04 us
    all_to_all x1, starting transfers between devices, on_device(): columns = jnp.concatenate(lax.all_to_all(sent, 'tp', 0, 0), axis=0)  5.83 us
  transfers between devices with their start and end apart: 4, of which 2 were waited for; matrix products, arithmetic and copies ran while one was open for 23% of the time, Pallas kernels for 0%

profile of v1, /device:TPU:0, one launch (start us, length us, event | category | flops | bytes accessed | tf_op | source)
XLA Modules:
  0.0 160.6 jit_solution(6959744360783251849)
XLA Ops:
  7.2 0.0 all-gather.2.cloned.1.call-start
  7.2 2.2 %fusion.12 = (bf16[192,1792]{1,0:T(8,128)(2,1)S(1)}, bf16[192,1792]{1,0:T(8,128)(2,1)S(1)}) fusion(bf16[192,1792]{1,0:T(8,128)(2,1)} %param.7, bf16[192,1792]{1,0:T(8,128)(2,1)} %param.8, bf16[192,1792]{1,0:T(8,128)(2,1)} %param.9), kind=kLoop, calls=%fused_computation.17 | loop fusion | flops 5505024 | bytes 3440640 | tf_op jit(solution)/shard_map/convert_element_type | solution.py:17
  9.4 0.0 copy-start
  9.5 1.2 pad_maximum_fusion
  10.6 0.0 all-gather.2.cloned.1.call-update
  10.7 9.3 %all_to_all.40 = bf16[24,4,1024]{2,0,1:T(8,128)(2,1)S(1)} all-to-all(bf16[24,4,1024]{2,0,1:T(8,128)(2,1)S(1)} %bitcast.34), channel_id=1, replica_groups=mesh['tp'=8,'dp'=4] {'dp'}, dimensions={1} | all-to-all | bytes 393216 | tf_op jit(solution)/shard_map/all_to_all | solution.py:22
  20.0 1.3 stack.5
  21.4 5.8 %all-to-all-start.2 = ((bf16[8,96,1024]{2,1,0:T(8,128)(2,1)}), bf16[8,96,1024]{2,1,0:T(8,128)(2,1)S(1)}, u32[]{:S(2)}, u32[]{:S(2)}) async-start(bf16[8,96,1024]{2,1,0:T(8,128)(2,1)} %stack.5), calls=%async_computation.3 | async-start | bytes 3145728 | tf_op jit(solution)/shard_map/all_to_all | solution.py:24
  27.2 0.0 reduce-scatter.2.cloned.1.call-start
  27.2 28.2 %all-gather.2.cloned.1.call-done = bf16[768,3584]{1,0:T(8,128)(2,1)} async-done(((bf16[192,3584]{1,0:T(8,128)(2,1)}), bf16[768,3584]{1,0:T(8,128)(2,1)}) %all-gather.2.cloned.1.call-update) | async-done | bytes 5505040 | tf_op jit(solution)/shard_map/all_gather | solution.py:21
  55.4 6.0 %fusion.3 = f32[768,1024]{1,0:T(8,128)S(1)} fusion(bf16[1024,1792]{1,0:T(8,128)(2,1)} %param.11, bf16[768,3584]{1,0:T(8,128)(2,1)} %all-gather.2.cloned.1.call-done), kind=kOutput, calls=%fused_computation.6 | convolution fusion | flops 2818572288 | bytes 9568256 | tf_op jit(solution)/shard_map/dot_general | solution.py:33
  61.5 3.0 %add_convert_fusion = bf16[768,1024]{1,0:T(8,128)(2,1)S(1)} fusion(f32[768,1024]{1,0:T(8,128)S(1)} %fusion.3, bf16[1024,1792]{1,0:T(8,128)(2,1)S(1)} %copy-done.2, bf16[768,3584]{1,0:T(8,128)(2,1)S(1)} %copy-done.1), kind=kOutput, calls=%fused_computation.4 | convolution fusion | flops 2820145152 | bytes 11141120 | tf_op jit(solution)/shard_map/dot_general | solution.py:30
  64.5 1.3 copy.20
  65.8 0.0 reduce-scatter.2.cloned.1.call-update
  65.8 0.0 all-to-all-done.2
  65.8 0.2 copy.23
  66.0 6.4 %fusion = bf16[1024,1792]{0,1:T(8,128)(2,1)} fusion(bf16[768,1024]{1,0:T(8,128)(2,1)S(1)} %bitcast.29, bf16[768,3584]{1,0:T(8,128)(2,1)} %all-gather.2.cloned.1.call-done), kind=kOutput, calls=%fused_computation.2 | convolution fusion | flops 2820407296 | bytes 7995392 | tf_op jit(solution)/shard_map/dot_general | solution.py:41
  72.4 59.1 %reduce-scatter.2.cloned.1.call-done = bf16[96,1024]{1,0:T(8,128)(2,1)} async-done(((bf16[768,1024]{1,0:T(8,128)(2,1)}), bf16[96,1024]{1,0:T(8,128)(2,1)}) %reduce-scatter.2.cloned.1.call-update) | async-done | bytes 196624 | tf_op jit(solution)/shard_map/reduce_scatter | solution.py:39
  131.5 3.4 %all-to-all-start = ((bf16[4,24,1024]{2,1,0:T(8,128)(2,1)}), bf16[4,24,1024]{2,1,0:T(8,128)(2,1)S(1)}, u32[]{:S(2)}, u32[]{:S(2)}) async-start(bf16[4,24,1024]{2,1,0:T(8,128)(2,1)} %bitcast.36), calls=%async_computation.1 | async-start | bytes 393216 | tf_op jit(solution)/shard_map/all_to_all | solution.py:40
  134.9 6.3 %fusion.1 = bf16[1024,1792]{0,1:T(8,128)(2,1)} fusion(bf16[768,1024]{1,0:T(8,128)(2,1)S(1)} %bitcast.30, bf16[768,3584]{1,0:T(8,128)(2,1)} %all-gather.2.cloned.1.call-done), kind=kOutput, calls=%fused_computation.3 | convolution fusion | flops 2820407296 | bytes 7995392 | tf_op jit(solution)/shard_map/dot_general | solution.py:44
  141.2 5.9 %copy.25 = bf16[1024,1792]{1,0:T(8,128)(2,1)} copy(bf16[1024,1792]{0,1:T(8,128)(2,1)} %fusion.1) | data formatting | bytes 7340032
  147.1 5.9 %copy.24 = bf16[1024,1792]{1,0:T(8,128)(2,1)} copy(bf16[1024,1792]{0,1:T(8,128)(2,1)} %fusion) | data formatting | bytes 7340032
  153.0 0.0 all-to-all-done
  153.0 0.7 copy.27
  (6 shorter events, 0.0 us)
Async XLA Ops:
  7.2 48.3 %all-gather.2.cloned.1.call-start = ((), (), s32[]{:S(2)}) async-start(), calls=%async_computation.4 | async-start | bytes 6881280 | tf_op jit(solution)/shard_map/all_gather | solution.py:21
  9.4 1.2 copy-start
  21.4 44.5 %all-to-all-start.2 = ((bf16[8,96,1024]{2,1,0:T(8,128)(2,1)}), bf16[8,96,1024]{2,1,0:T(8,128)(2,1)S(1)}, u32[]{:S(2)}, u32[]{:S(2)}) async-start(bf16[8,96,1024]{2,1,0:T(8,128)(2,1)} %stack.5), calls=%async_computation.3 | async-start | bytes 3145728 | tf_op jit(solution)/shard_map/all_to_all | solution.py:24
  27.2 104.3 %reduce-scatter.2.cloned.1.call-start = ((), (), s32[]{:S(2)}) async-start(), calls=%async_computation.5 | async-start | bytes 1769472 | tf_op jit(solution)/shard_map/reduce_scatter | solution.py:39
  55.4 6.1 %copy-start.1 = (bf16[768,3584]{1,0:T(8,128)(2,1)S(1)}, bf16[768,3584]{1,0:T(8,128)(2,1)}, u32[]{:S(2)}) copy-start(bf16[768,3584]{1,0:T(8,128)(2,1)} %all-gather.2.cloned.1.call-done) | copy-start | bytes 16515076
  55.4 6.1 %copy-start.2 = (bf16[1024,1792]{1,0:T(8,128)(2,1)S(1)}, bf16[1024,1792]{1,0:T(8,128)(2,1)}, u32[]{:S(2)}) copy-start(bf16[1024,1792]{1,0:T(8,128)(2,1)} %param.10) | copy-start | bytes 11010052
  131.5 21.5 %all-to-all-start = ((bf16[4,24,1024]{2,1,0:T(8,128)(2,1)}), bf16[4,24,1024]{2,1,0:T(8,128)(2,1)S(1)}, u32[]{:S(2)}, u32[]{:S(2)}) async-start(bf16[4,24,1024]{2,1,0:T(8,128)(2,1)} %bitcast.36), calls=%async_computation.1 | async-start | bytes 393216 | tf_op jit(solution)/shard_map/all_to_all | solution.py:40
Sparse Core Ops, SparseCore 0:
  10.8 44.6 all-gather.1
  65.9 65.5 reduce-scatter.1
